TPU v7x, 128 devices: a whole 4x4x4 slice. The times are simulated.
128 devices in a mesh: rep: 1, dp: 128 (over x, y, z, core).
Axes of the slice: x: 4, y: 4, z: 4, core: 2. Of those that a mesh axis runs over, the one named last changes fastest.
Arguments:
- a: bfloat16 [128, 2, 4096, 1024], P(('rep', 'dp'))
- g: bfloat16 [128, 2, 4096, 3200], P(('rep', 'dp'))
Outputs:
- output: bfloat16 [2, 1024, 3200], P('rep')
All inputs are finite; a program needn't handle non-finite values.
Results may differ from a plain program's by a relative error of at most 0.012.
Values are sent between devices in bfloat16 or wider.
A program may use at most 1.5 GiB of HBM per device.

v0:
```python
import jax
import jax.numpy as jnp


def solution(mesh):
    groups = mesh.shape["rep"]

    def step(a, g):
        a, g = (t.reshape(groups, -1, *t.shape[1:]) for t in (a, g))
        sums = jnp.einsum("rsntd,rsntf->rndf", a, g, preferred_element_type=jnp.float32)
        return sums.astype(jnp.bfloat16).reshape(-1, *sums.shape[2:])

    return step
```

profile of v0, /device:TPU:1, one launch (start us, length us, event | category | flops | bytes accessed | tf_op | source)
XLA Modules:
  0.0 236.4 jit_solution(4356614652080805556)
XLA Ops:
  0.0 67.8 %fusion = f32[2,1024,3200]{2,1,0:T(8,128)} fusion(bf16[1,2,4096,3200]{3,2,1,0:T(8,128)(2,1)} %param.1, bf16[1,2,4096,1024]{3,2,1,0:T(8,128)(2,1)} %param), kind=kOutput, calls=%fused_computation | convolution fusion | flops 53687091200 | bytes 95420416 | tf_op jit(solution)/rsntd,rsntf->rndf/dot_general | solution.py:10
  67.8 168.6 %all-reduce.2 = bf16[2,1024,3200]{2,1,0:T(8,128)(2,1)} all-reduce(f32[2,1024,3200]{2,1,0:T(8,128)} %fusion), channel_id=1, replica_groups=mesh['axis_0'=128] {'axis_0'}, use_global_device_ids=true, to_apply=%add.clone | all-reduce | flops 6553600 | bytes 39321600 | tf_op jit(solution)/rsntd,rsntf->rndf/dot_general | solution.py:10
where the time goes:
time: 238 us; the launch traced here: 236 us
  blocking collectives  169 us (71%)
  matrix products  67.8 us (28%)
    dot_general x1, blocking collectives, step(): jnp.einsum('rsntd,rsntf->rndf', a, g, preferred_element_type=jnp.float32)  169 us
    dot_general x1, matrix products, step(): jnp.einsum('rsntd,rsntf->rndf', a, g, preferred_element_type=jnp.float32)  67.8 us

commit v1 on v0

v1 whole, which is shorter than its diff:
```python
import jax
import jax.numpy as jnp
from jax import lax
from jax.experimental import pallas as pl
from jax.experimental.pallas import tpu as pltpu
from jax.sharding import PartitionSpec as P

BF, F32 = jnp.bfloat16, jnp.float32
MESH = pl.DeviceIdType.MESH
N, T, D, FF = 2, 4096, 1024, 3200
W = 256
PER = FF // W
NT = N * PER + 1
R = 8
LAG = (0, 1, 3, 5, 7, 9, 11, 13, 15, 17, 18)
CH = 512
NA = 4


def rows(start, size, unit):
    return pl.ds(pl.multiple_of(start, unit), size)


def kernel(a_ref, g_ref, out, raw, at, gb, acc, q2, q3, b0, b1a, b1b, b2, b3, r0, r1a, r1b, r2, r3,
           sem_a, sem_g, s0, s1a, s1b, s2, s3, t3, t2, t1a, t1b, t0, d0, d1a, d1b, d2, d3, e3, e2, e1a, e1b, e0):
    me = lax.axis_index("dp")
    c = lax.rem(me, 2)
    mate = me + 1 - 2 * c

    def ring(i, stage):
        axis = lax.rem(i + stage, 3)
        stride = jnp.where(axis == 0, 32, jnp.where(axis == 1, 8, 2))
        return stride, lax.rem(lax.div(me, stride), 4)

    def peer(r, d):
        stride, v = r
        return me + (lax.rem(v + d, 4) - v) * stride

    def send(src, dst, send_sem, recv_sem, to):
        return pltpu.make_async_remote_copy(src_ref=src, dst_ref=dst, send_sem=send_sem, recv_sem=recv_sem,
                                            device_id={"dp": to}, device_id_type=MESH)

    def block(i, h):
        last = i == NT - 1
        n = jnp.where(last, h, lax.div(i, PER))
        col = jnp.where(last, PER * W, lax.rem(i, PER) * W + h * 128)
        return n, pl.ds(pl.multiple_of(col, 128), 128)

    def c0(i):
        s = lax.rem(i, R)
        return [send(b0.at[s], r0.at[i], s0.at[s], d0.at[i], mate)]

    def c1a(i):
        s, r = lax.rem(i, R), ring(i, 0)
        return [send(b1a.at[s, k], r1a.at[i, k], s1a.at[s, k], d1a.at[i, k], peer(r, d)) for k, d in ((0, 1), (1, 3))]

    def c1b(i):
        s, r = lax.rem(i, R), ring(i, 0)
        return [send(b1b.at[s, k], r1b.at[i, k], s1b.at[s, k], d1b.at[i, k], peer(r, d)) for k, d in ((0, 1), (1, 3))]

    def c2(i):
        s, r = lax.rem(i, R), ring(i, 1)
        return [send(b2.at[s, k], r2.at[i, k], s2.at[s, k], d2.at[i, k], peer(r, k + 1)) for k in range(3)]

    def c3(i):
        s, r = lax.rem(i, R), ring(i, 2)
        return [send(b3.at[s, k], r3.at[i, k], s3.at[s, k], d3.at[i, k], peer(r, k + 1)) for k in range(3)]

    def part(i, start, size):
        n, cols = block(i, c)
        return out.at[n, rows(start, size, size), cols]

    def gather(i, start, size, r, d, ss, rs):
        return send(part(i, start, size), part(i, start, size), ss, rs, peer(r, d))

    def f3(i):
        s, x1, x2, x3 = lax.rem(i, R), ring(i, 0), ring(i, 1), ring(i, 2)
        return [gather(i, 256 * x1[1] + 64 * x2[1] + 16 * x3[1], 16, x3, k + 1, t3.at[s, k], e3.at[i, k]) for k in range(3)]

    def f2(i):
        s, x1, x2 = lax.rem(i, R), ring(i, 0), ring(i, 1)
        return [gather(i, 256 * x1[1] + 64 * x2[1], 64, x2, k + 1, t2.at[s, k], e2.at[i, k]) for k in range(3)]

    def f1a(i):
        s, x1 = lax.rem(i, R), ring(i, 0)
        return [gather(i, 256 * x1[1], 256, x1, d, t1a.at[s, k], e1a.at[i, k]) for k, d in ((0, 1), (1, 3))]

    def f1b(i):
        s, x1 = lax.rem(i, R), ring(i, 0)
        return [gather(i, 256 * lax.rem(x1[1] + 4 - d, 4) + 128 * k, 128, x1, d, t1b.at[s, k], e1b.at[i, k])
                for k, d in ((0, 1), (1, 3))]

    def f0(i, which):
        s, x1 = lax.rem(i, R), ring(i, 0)
        return [send(part(i, 256 * lax.rem(x1[1] + d, 4), 256), part(i, 256 * lax.rem(x1[1] + d, 4), 256), t0.at[s, k], e0.at[i, k], mate)
                for k, d in ((0, 0), (1, 3), (2, 1), (3, 2)) if k in which]

    def start(copies):
        for x in copies:
            x.start()

    def arrived(copies):
        for x in copies:
            x.wait_recv()

    def sent(copies):
        for x in copies:
            x.wait_send()

    def gcopies(i):
        s = lax.rem(i, 2)
        n, j = lax.div(i, PER), lax.rem(i, PER)
        return [pltpu.make_async_copy(g_ref.at[0, n, :, pl.ds(pl.multiple_of(j * W, 128), W)], gb.at[s], sem_g.at[s])]

    def glast():
        s = (NT - 1) % 2
        return [pltpu.make_async_copy(g_ref.at[0, n, :, pl.ds(PER * W, 128)], gb.at[s, :, pl.ds(128 * n, 128)], sem_g.at[2 * n])
                for n in range(N)]

    def acopy(i):
        s = lax.rem(i, NA)
        n, j = lax.div(i, T // CH), lax.rem(i, T // CH)
        return pltpu.make_async_copy(a_ref.at[0, n, rows(j * CH, CH, CH)], raw.at[s], sem_a.at[s])

    for k in range(NA - 1):
        acopy(k).start()
    start(gcopies(0))

    barrier = pltpu.get_barrier_semaphore()
    pl.semaphore_signal(barrier, inc=1, device_id={"dp": mate}, device_id_type=MESH)
    for axis in range(3):
        for d in (1, 2, 3):
            pl.semaphore_signal(barrier, inc=1, device_id={"dp": peer(ring(axis, 0), d)}, device_id_type=MESH)
    pl.semaphore_wait(barrier, 10)

    def transpose(i, carry):
        @pl.when(i + NA - 1 < N * T // CH)
        def _():
            acopy(i + NA - 1).start()

        acopy(i).wait()
        n, j = lax.div(i, T // CH), lax.rem(i, T // CH)
        at[n, :, pl.ds(pl.multiple_of(j * CH, CH), CH)] = raw[lax.rem(i, NA)].T
        return carry

    lax.fori_loop(0, N * T // CH, transpose, 0)

    def e_0(i):
        s = lax.rem(i, R)
        slot = lax.rem(i, 2)

        @pl.when(i < NT - 2)
        def _():
            start(gcopies(i + 1))

        @pl.when(i == NT - 2)
        def _():
            start(glast())

        @pl.when(i < NT - 1)
        def _():
            n = lax.div(i, PER)
            arrived_g = gcopies(i)
            arrived_g[0].wait()
            r = jnp.dot(at[n], gb[slot], preferred_element_type=F32)
            acc[s, 0] = r[:, :128]
            acc[s, 1] = r[:, 128:]

        @pl.when(i == NT - 1)
        def _():
            for x in glast():
                x.wait()
            for n in range(N):
                acc[s, n] = jnp.dot(at[n], gb[(NT - 1) % 2, :, 128 * n : 128 * n + 128], preferred_element_type=F32)

        b0[s] = acc[s, 1 - c].astype(BF)
        start(c0(i))

    def e_1(i):
        s, (_, v) = lax.rem(i, R), ring(i, 0)
        arrived(c0(i))
        acc[s, c] = acc[s, c] + r0[i].astype(F32)
        p = lax.rem(v + 2, 4) * 256
        for k in range(2):
            b1a[s, k] = acc[s, c, rows(p + 128 * k, 128, 128)].astype(BF)
        start(c1a(i))

    def e_2(i):
        s, (_, v) = lax.rem(i, R), ring(i, 0)
        sent(c0(i))
        arrived(c1a(i))
        for k, d in ((0, 1), (1, 3)):
            p = lax.rem(v + d, 4) * 256
            b1b[s, k, 128 * k : 128 * k + 128] = (acc[s, c, rows(p + 128 * k, 128, 128)] + r1a[i, k].astype(F32)).astype(BF)
            o = 1 - k
            b1b[s, k, 128 * o : 128 * o + 128] = acc[s, c, rows(p + 128 * o, 128, 128)].astype(BF)
        start(c1b(i))

    def e_3(i):
        s, (_, v), (_, w) = lax.rem(i, R), ring(i, 0), ring(i, 1)
        sent(c1a(i))
        arrived(c1b(i))
        q2[s] = acc[s, c, rows(v * 256, 256, 256)] + r1b[i, 0].astype(F32) + r1b[i, 1].astype(F32)
        for k in range(3):
            b2[s, k] = q2[s, rows(lax.rem(w + k + 1, 4) * 64, 64, 64)].astype(BF)
        start(c2(i))

    def e_4(i):
        s, (_, w), (_, u) = lax.rem(i, R), ring(i, 1), ring(i, 2)
        sent(c1b(i))
        arrived(c2(i))
        q3[s] = q2[s, rows(w * 64, 64, 64)] + r2[i, 0].astype(F32) + r2[i, 1].astype(F32) + r2[i, 2].astype(F32)
        for k in range(3):
            b3[s, k] = q3[s, rows(lax.rem(u + k + 1, 4) * 16, 16, 16)].astype(BF)
        start(c3(i))

    def e_5(i):
        s, (_, v), (_, w), (_, u) = lax.rem(i, R), ring(i, 0), ring(i, 1), ring(i, 2)
        sent(c2(i))
        arrived(c3(i))
        n, cols = block(i, c)
        total = q3[s, rows(u * 16, 16, 16)] + r3[i, 0].astype(F32) + r3[i, 1].astype(F32) + r3[i, 2].astype(F32)
        out[n, rows(256 * v + 64 * w + 16 * u, 16, 16), cols] = total.astype(BF)
        start(f3(i))

    def e_6(i):
        sent(c3(i))
        arrived(f3(i))
        start(f2(i))

    def e_7(i):
        sent(f3(i))
        arrived(f2(i))
        start(f1a(i))
        start(f0(i, (0,)))

    def e_8(i):
        sent(f2(i))
        arrived(f1a(i))
        start(f1b(i))
        start(f0(i, (1, 2)))

    def e_9(i):
        sent(f1a(i))
        arrived(f1b(i))
        start(f0(i, (3,)))

    def e_10(i):
        sent(f1b(i))
        for x in f0(i, (0, 1, 2, 3)):
            x.wait_send()
            x.wait_recv()

    steps = (e_0, e_1, e_2, e_3, e_4, e_5, e_6, e_7, e_8, e_9, e_10)

    def iteration(t, carry):
        for lag, step in zip(LAG, steps):
            i = t - lag

            @pl.when((i >= 0) & (i < NT))
            def _(i=i, step=step):
                step(i)

        return carry

    lax.fori_loop(0, NT + LAG[-1], iteration, 0)


def solution(mesh):
    dma = pltpu.SemaphoreType.DMA

    def step(a, g):
        return pl.pallas_call(
            kernel,
            out_shape=jax.ShapeDtypeStruct((N, D, FF), BF),
            in_specs=[pl.BlockSpec(memory_space=pl.ANY)] * 2,
            out_specs=pl.BlockSpec(memory_space=pltpu.VMEM),
            scratch_shapes=[
                pltpu.VMEM((NA, CH, D), BF), pltpu.VMEM((N, D, T), BF), pltpu.VMEM((2, T, W), BF),
                pltpu.VMEM((R, 2, D, 128), F32), pltpu.VMEM((R, 256, 128), F32), pltpu.VMEM((R, 64, 128), F32),
                pltpu.VMEM((R, D, 128), BF), pltpu.VMEM((R, 2, 128, 128), BF), pltpu.VMEM((R, 2, 256, 128), BF),
                pltpu.VMEM((R, 3, 64, 128), BF), pltpu.VMEM((R, 3, 16, 128), BF),
                pltpu.VMEM((NT, D, 128), BF), pltpu.VMEM((NT, 2, 128, 128), BF), pltpu.VMEM((NT, 2, 256, 128), BF),
                pltpu.VMEM((NT, 3, 64, 128), BF), pltpu.VMEM((NT, 3, 16, 128), BF),
                dma((NA,)), dma((3,)),
                dma((R,)), dma((R, 2)), dma((R, 2)), dma((R, 3)), dma((R, 3)),
                dma((R, 3)), dma((R, 3)), dma((R, 2)), dma((R, 2)), dma((R, 4)),
                dma((NT,)), dma((NT, 2)), dma((NT, 2)), dma((NT, 3)), dma((NT, 3)),
                dma((NT, 3)), dma((NT, 3)), dma((NT, 2)), dma((NT, 2)), dma((NT, 4)),
            ],
            compiler_params=pltpu.CompilerParams(collective_id=0, has_side_effects=True, vmem_limit_bytes=67043328),
        )(a, g)

    return jax.shard_map(step, mesh=mesh, in_specs=(P(("rep", "dp")), P(("rep", "dp"))), out_specs=P("rep"), check_vma=False)
```

time: 238 us -> 145 us (0.61)
  blocking collectives: 169 us -> 0 us
  Pallas kernels: 0 us -> 134 us
  matrix products: 67.8 us -> 0 us
  local copies, waits for them, and re-layouts: 0 us -> 10.8 us
    dot_general x1 -> x0, blocking collectives: 169 us -> none  [step(): jnp.einsum('rsntd,rsntf->rndf', a, g, preferred_element_type=jnp.float32)]
    pallas_call x0 -> x1, Pallas kernels: none -> 134 us  [step(): pl.pallas_call(kernel, out_shape=jax.ShapeDtypeStruct((N, D, FF), BF), in...]
    dot_general x1 -> x0, matrix products: 67.8 us -> none  [step(): jnp.einsum('rsntd,rsntf->rndf', a, g, preferred_element_type=jnp.float32)]
    unnamed x0 -> x1, local copies, waits for them, and re-layouts: none -> 10.8 us
where the time goes in v1:
time: 145 us
  Pallas kernels  134 us (92%)
  local copies, waits for them, and re-layouts  10.8 us (7%)
    pallas_call x1, Pallas kernels, step(): pl.pallas_call(kernel, out_shape=jax.ShapeDtypeStruct((N, D, FF), BF), in...  134 us
    unnamed x1, local copies, waits for them, and re-layouts  10.8 us

profile of v1, /device:TPU:1, one launch (start us, length us, event | category | flops | bytes accessed | tf_op | source)
XLA Modules:
  0.0 145.0 jit_solution(17647701909348120814)
XLA Ops:
  0.0 134.2 %shard_map.28 = bf16[2,1024,3200]{2,1,0:T(8,128)(2,1)} custom-call(bf16[1,2,4096,1024]{3,2,1,0:T(8,128)(2,1)} %a_ref.1, bf16[1,2,4096,3200]{3,2,1,0:T(8,128)(2,1)} %g_ref.1), custom_call_target="tpu_custom_call" | custom-call | tf_op jit(solution)/shard_map/pallas_call | solution.py:273
  134.2 10.8 %copy.4 = bf16[2,1024,3200]{2,1,0:T(8,128)(2,1)} copy(bf16[2,1024,3200]{2,1,0:T(8,128)(2,1)} %shard_map.28) | data formatting | bytes 26214400

commit v2 on v1

v2 whole, which is shorter than its diff:
```python
import jax
import jax.numpy as jnp
from jax import lax
from jax.experimental import pallas as pl
from jax.experimental.pallas import tpu as pltpu
from jax.sharding import PartitionSpec as P

BF, F32 = jnp.bfloat16, jnp.float32
MESH = pl.DeviceIdType.MESH
N, T, D, FF = 2, 4096, 1024, 3200
W = 256
PER = FF // W
NT = N * PER + 1
OWN = NT // 2 + 1
R = 4
LAG = (0, 1, 3, 5, 7, 9, 11, 13, 15, 16)
CH = 512
BLOCKS = T // CH
NA = 4


def rows(start, size, unit):
    return pl.ds(pl.multiple_of(start, unit), size)


def kernel(a_ref, g_ref, out, raw, at, gb, acc, q2, b0, b1a, b1b, b2, r0, r1a, r1b, r2, r3,
           sem_a, sem_g, s0, s1a, s1b, s2, s3, t2, t1a, t1b, t0, d0, d1a, d1b, d2, d3, e2, e1a, e1b, e0):
    me = lax.axis_index("dp")
    c = lax.rem(me, 2)
    mate = me + 1 - 2 * c

    def owner(i):
        return jnp.where(i >= NT - 2, 1, jnp.where(i == NT - 3, 0, 1 - lax.rem(i, 2)))

    def ring(i, stage):
        axis = lax.rem(i + stage, 3)
        stride = jnp.where(axis == 0, 32, jnp.where(axis == 1, 8, 2))
        return stride, lax.rem(lax.div(me, stride), 4)

    def peer(r, d):
        stride, v = r
        return me + (lax.rem(v + d, 4) - v) * stride

    def send(src, dst, send_sem, recv_sem, to):
        return pltpu.make_async_remote_copy(src_ref=src, dst_ref=dst, send_sem=send_sem, recv_sem=recv_sem,
                                            device_id={"dp": to}, device_id_type=MESH)

    def slots(i):
        j = lax.div(i, 2)
        return j, lax.rem(j, R)

    def c0(i):
        j, s = slots(i)
        return [send(b0.at[s], r0.at[j], s0.at[s], d0.at[j], mate)]

    def c1a(i):
        (j, s), r = slots(i), ring(i, 0)
        return [send(b1a.at[s, k], r1a.at[j, k], s1a.at[s, k], d1a.at[j, k], peer(r, d)) for k, d in ((0, 1), (1, 3))]

    def c1b(i):
        (j, s), r = slots(i), ring(i, 0)
        return [send(b1b.at[s, k], r1b.at[j, k], s1b.at[s, k], d1b.at[j, k], peer(r, d)) for k, d in ((0, 1), (1, 3))]

    def c2(i):
        (j, s), r = slots(i), ring(i, 1)
        return [send(b2.at[s, k], r2.at[j, k], s2.at[s, k], d2.at[j, k], peer(r, k + 1)) for k in range(3)]

    def c3(i):
        (j, s), r = slots(i), ring(i, 2)
        return [send(r3.at[j, r[1]], r3.at[j, r[1]], s3.at[s, k], d3.at[j, k], peer(r, k + 1)) for k in range(3)]

    def gather(i, start, size, to, ss, rs):
        piece = out.at[i, rows(start, size, size)]
        return send(piece, piece, ss, rs, to)

    def f2(i):
        (j, s), x1, x2 = slots(i), ring(i, 0), ring(i, 1)
        return [gather(i, 256 * x1[1] + 64 * x2[1], 64, peer(x2, k + 1), t2.at[s, k], e2.at[j, k]) for k in range(3)]

    def f1a(i):
        (j, s), x1 = slots(i), ring(i, 0)
        return [gather(i, 256 * x1[1], 256, peer(x1, d), t1a.at[s, k], e1a.at[j, k]) for k, d in ((0, 1), (1, 3))]

    def f1b(i):
        (j, s), x1 = slots(i), ring(i, 0)
        return [gather(i, 256 * lax.rem(x1[1] + 4 - d, 4) + 128 * k, 128, peer(x1, d), t1b.at[s, k], e1b.at[j, k])
                for k, d in ((0, 1), (1, 3))]

    def f0(i, which):
        (j, s), x1 = slots(i), ring(i, 0)
        return [gather(i, 256 * lax.rem(x1[1] + d, 4), 256, mate, t0.at[s, k], e0.at[i, k])
                for k, d in ((0, 0), (1, 3), (2, 1), (3, 2)) if k in which]

    def start(copies):
        for x in copies:
            x.start()

    def arrived(copies):
        for x in copies:
            x.wait_recv()

    def sent(copies):
        for x in copies:
            x.wait_send()

    def gcopy(i):
        s = lax.rem(i, 2)
        n, j = lax.div(i, PER), lax.rem(i, PER)
        return pltpu.make_async_copy(g_ref.at[0, n, :, pl.ds(pl.multiple_of(j * W, W), W)], gb.at[s], sem_g.at[s, 0])

    def glast():
        s = (NT - 1) % 2
        return [pltpu.make_async_copy(g_ref.at[0, n, :, pl.ds(PER * W, 128)], gb.at[s, :, pl.ds(128 * n, 128)], sem_g.at[s, n])
                for n in range(N)]

    def acopy(k):
        s = lax.rem(k, NA)
        n, j = lax.div(k, BLOCKS), lax.rem(k, BLOCKS)
        return pltpu.make_async_copy(a_ref.at[0, n, rows(j * CH, CH, CH)], raw.at[s], sem_a.at[s])

    barrier = pltpu.get_barrier_semaphore()
    pl.semaphore_signal(barrier, inc=1, device_id={"dp": mate}, device_id_type=MESH)
    for axis in range(3):
        for d in (1, 2, 3):
            pl.semaphore_signal(barrier, inc=1, device_id={"dp": peer(ring(axis, 0), d)}, device_id_type=MESH)

    for k in range(NA - 1):
        acopy(k).start()
    gcopy(0).start()

    def transpose(k):
        @pl.when(k + NA - 1 < N * BLOCKS)
        def _():
            acopy(k + NA - 1).start()

        acopy(k).wait()
        n, j = lax.div(k, BLOCKS), lax.rem(k, BLOCKS)
        at[n, :, rows(j * CH, CH, CH)] = raw[lax.rem(k, NA)].T

    def first(k, carry):
        transpose(k)
        return carry

    lax.fori_loop(0, BLOCKS, first, 0)
    pl.semaphore_wait(barrier, 10)

    def tile(i, mine):
        _, s = slots(i)
        slot = lax.rem(i, 2)

        @pl.when(i < NT - 1)
        def _():
            r = jnp.dot(at[lax.div(i, PER)], gb[slot], preferred_element_type=F32)
            if mine:
                acc[s] = r
            else:
                b0[s] = r.astype(BF)

        @pl.when(i == NT - 1)
        def _():
            for n in range(N):
                cols = slice(128 * n, 128 * n + 128)
                r = jnp.dot(at[n], gb[slot, :, cols], preferred_element_type=F32)
                if mine:
                    acc[s, :, cols] = r
                else:
                    b0[s, :, cols] = r.astype(BF)

    def e_0(i, mine):
        @pl.when(i < NT - 2)
        def _():
            gcopy(i + 1).start()

        @pl.when(i == NT - 2)
        def _():
            start(glast())

        @pl.when(i < NT - 1)
        def _():
            gcopy(i).wait()

        @pl.when(i == NT - 1)
        def _():
            for x in glast():
                x.wait()

        @pl.when(mine)
        def _():
            tile(i, True)

        @pl.when(jnp.logical_not(mine))
        def _():
            tile(i, False)
            start(c0(i))

        @pl.when(i < BLOCKS)
        def _():
            transpose(i + BLOCKS)

    def pair(i, at_row, size):
        j, s = slots(i)
        return acc[s, rows(at_row, size, size)] + r0[j, rows(at_row, size, size)].astype(F32)

    def e_1(i):
        (j, s), (_, v) = slots(i), ring(i, 0)
        arrived(c0(i))
        p = lax.rem(v + 2, 4) * 256
        for k in range(2):
            b1a[s, k] = pair(i, p + 128 * k, 128).astype(BF)
        start(c1a(i))

    def e_2(i):
        (j, s), (_, v) = slots(i), ring(i, 0)
        arrived(c1a(i))
        for k, d in ((0, 1), (1, 3)):
            p, o = lax.rem(v + d, 4) * 256, 1 - k
            b1b[s, k, 128 * k : 128 * k + 128] = (pair(i, p + 128 * k, 128) + r1a[j, k].astype(F32)).astype(BF)
            b1b[s, k, 128 * o : 128 * o + 128] = pair(i, p + 128 * o, 128).astype(BF)
        start(c1b(i))

    def e_3(i):
        (j, s), (_, v), (_, w) = slots(i), ring(i, 0), ring(i, 1)
        sent(c1a(i))
        arrived(c1b(i))
        q2[s] = pair(i, v * 256, 256) + r1b[j, 0].astype(F32) + r1b[j, 1].astype(F32)
        for k in range(3):
            b2[s, k] = q2[s, rows(lax.rem(w + k + 1, 4) * 64, 64, 64)].astype(BF)
        start(c2(i))

    def e_4(i):
        (j, s), (_, w), (_, u) = slots(i), ring(i, 1), ring(i, 2)
        sent(c1b(i))
        arrived(c2(i))
        partial = q2[s, rows(w * 64, 64, 64)] + r2[j, 0].astype(F32) + r2[j, 1].astype(F32) + r2[j, 2].astype(F32)
        r3[j, u] = partial.astype(BF)
        start(c3(i))

    def e_5(i):
        (j, s), (_, v), (_, w) = slots(i), ring(i, 0), ring(i, 1)
        sent(c2(i))
        arrived(c3(i))
        total = r3[j, 0].astype(F32) + r3[j, 1].astype(F32) + r3[j, 2].astype(F32) + r3[j, 3].astype(F32)
        out[i, rows(256 * v + 64 * w, 64, 64)] = total.astype(BF)
        start(f2(i))

    def e_6(i):
        sent(c3(i))
        arrived(f2(i))
        start(f1a(i))
        start(f0(i, (0,)))

    def e_7(i):
        sent(f2(i))
        arrived(f1a(i))
        start(f1b(i))
        start(f0(i, (1, 2)))

    def e_8(i):
        sent(f1a(i))
        arrived(f1b(i))
        start(f0(i, (3,)))

    def e_9(i):
        sent(f1b(i))
        sent(f0(i, (0, 1, 2, 3)))

    owned = (e_1, e_2, e_3, e_4, e_5, e_6, e_7, e_8, e_9)

    def iteration(t, carry):
        @pl.when(t < NT)
        def _():
            e_0(t, owner(t) == c)

        for lag, step in zip(LAG[1:], owned):
            i = t - lag
            inside = (i >= 0) & (i < NT)

            @pl.when(inside & (owner(i) == c))
            def _(i=i, step=step):
                step(i)

            if step is e_2 or step is e_9:
                @pl.when(inside & (owner(i) != c))
                def _(i=i, step=step):
                    if step is e_2:
                        sent(c0(i))
                    else:
                        arrived(f0(i, (0, 1, 2, 3)))

        return carry

    lax.fori_loop(0, NT + LAG[-1], iteration, 0)


def store(x, out, sems):
    copies = [pltpu.make_async_copy(x.at[i], out.at[i // PER, :, pl.ds(i % PER * W, W)], sems.at[i]) for i in range(NT - 1)]
    copies += [pltpu.make_async_copy(x.at[NT - 1, :, pl.ds(128 * n, 128)], out.at[n, :, pl.ds(PER * W, 128)], sems.at[NT - 1 + n])
               for n in range(N)]
    for y in copies:
        y.start()
    for y in copies:
        y.wait()


def solution(mesh):
    dma = pltpu.SemaphoreType.DMA

    def step(a, g):
        sums = pl.pallas_call(
            kernel,
            out_shape=pltpu.VMEM((NT, D, W), BF),
            in_specs=[pl.BlockSpec(memory_space=pl.ANY)] * 2,
            out_specs=pl.BlockSpec(memory_space=pltpu.VMEM),
            scratch_shapes=[
                pltpu.VMEM((NA, CH, D), BF), pltpu.VMEM((N, D, T), BF), pltpu.VMEM((2, T, W), BF),
                pltpu.VMEM((R, D, W), F32), pltpu.VMEM((R, 256, W), F32),
                pltpu.VMEM((R, D, W), BF), pltpu.VMEM((R, 2, 128, W), BF), pltpu.VMEM((R, 2, 256, W), BF),
                pltpu.VMEM((R, 3, 64, W), BF),
                pltpu.VMEM((OWN, D, W), BF), pltpu.VMEM((OWN, 2, 128, W), BF), pltpu.VMEM((OWN, 2, 256, W), BF),
                pltpu.VMEM((OWN, 3, 64, W), BF), pltpu.VMEM((OWN, 4, 64, W), BF),
                dma((NA,)), dma((2, 2)),
                dma((R,)), dma((R, 2)), dma((R, 2)), dma((R, 3)), dma((R, 3)),
                dma((R, 3)), dma((R, 2)), dma((R, 2)), dma((R, 4)),
                dma((OWN,)), dma((OWN, 2)), dma((OWN, 2)), dma((OWN, 3)), dma((OWN, 3)),
                dma((OWN, 3)), dma((OWN, 2)), dma((OWN, 2)), dma((NT, 4)),
            ],
            compiler_params=pltpu.CompilerParams(collective_id=0, has_side_effects=True, vmem_limit_bytes=50 * 1024 * 1024),
        )(a, g)
        return pl.pallas_call(
            store,
            out_shape=jax.ShapeDtypeStruct((N, D, FF), BF),
            in_specs=[pl.BlockSpec(memory_space=pltpu.VMEM)],
            out_specs=pl.BlockSpec(memory_space=pl.ANY),
            scratch_shapes=[dma((NT + 1,))],
            compiler_params=pltpu.CompilerParams(vmem_limit_bytes=1024 * 1024),
        )(sums)

    return jax.shard_map(step, mesh=mesh, in_specs=(P(("rep", "dp")), P(("rep", "dp"))), out_specs=P("rep"), check_vma=False)
```

time: 145 us -> 129 us (0.89)
  local copies, waits for them, and re-layouts: 10.8 us -> 0 us
  Pallas kernels: 134 us -> 128 us
    unnamed x1 -> x0, local copies, waits for them, and re-layouts: 10.8 us -> none
    pallas_call x1 -> x2, Pallas kernels: 134 us -> 128 us  [the longest x1 124 us: step(): pl.pallas_call(kernel, out_shape=pltpu.VMEM((NT, D, W), BF), in_specs=[pl...]
where the time goes in v2:
time: 129 us; the launch traced here: 128 us
  Pallas kernels  128 us (99%)
    pallas_call x1, Pallas kernels, step(): pl.pallas_call(kernel, out_shape=pltpu.VMEM((NT, D, W), BF), in_specs=[pl...  124 us
    pallas_call x1, Pallas kernels, step(): pl.pallas_call(store, out_shape=jax.ShapeDtypeStruct((N, D, FF), BF), in_...  4.91 us

profile of v2, /device:TPU:1, one launch (start us, length us, event | category | flops | bytes accessed | tf_op | source)
XLA Modules:
  0.0 128.5 jit_solution(14933614942847847954)
XLA Ops:
  0.0 123.6 %shard_map.28.x = bf16[25,1024,256]{2,1,0:T(8,128)(2,1)S(1)} custom-call(bf16[1,2,4096,1024]{3,2,1,0:T(8,128)(2,1)} %a_ref.1, bf16[1,2,4096,3200]{3,2,1,0:T(8,128)(2,1)} %g_ref.1), custom_call_target="tpu_custom_call" | custom-call | tf_op jit(solution)/shard_map/pallas_call | solution.py:309
  123.6 4.9 %shard_map.29 = bf16[2,1024,3200]{2,1,0:T(8,128)(2,1)} custom-call(bf16[25,1024,256]{2,1,0:T(8,128)(2,1)S(1)} %shard_map.28.x), custom_call_target="tpu_custom_call" | custom-call | tf_op jit(solution)/shard_map/pallas_call | solution.py:329

commit v3 on v2

v3 whole, which is shorter than its diff:
```python
import jax
import jax.numpy as jnp
from jax import lax
from jax.experimental import pallas as pl
from jax.experimental.pallas import tpu as pltpu
from jax.sharding import PartitionSpec as P

BF, F32 = jnp.bfloat16, jnp.float32
MESH = pl.DeviceIdType.MESH
N, T, D, FF = 2, 4096, 1024, 3200
W = 256
PER = FF // W
WHOLE = N * PER
NT = WHOLE + N
OWN = NT // 2 + 1
R = 4
LAG = (0, 1, 3, 6, 8, 10, 13, 16, 18, 19)
HALF = (128, 128)
FROM = (0, HALF[0])
CH = 512
BLOCKS = T // CH
NA = 4


def rows(start, size, unit):
    return pl.ds(pl.multiple_of(start, unit), size)


def kernel(a_ref, g_ref, out, raw, at, gb, acc, q2, b0, b1a, b1b, b2, r0, r1a, r1b, r2, r3,
           sem_a, sem_g, s0, s1a, s1b, s2, s3, t2, t1a, t1b, t0, d0, d1a, d1b, d2, d3, e2, e1a, e1b, e0):
    me = lax.axis_index("dp")
    c = lax.rem(me, 2)
    mate = me + 1 - 2 * c

    def owner(i):
        return jnp.where(i >= NT - 3, 1, jnp.where(i == NT - 4, 0, 1 - lax.rem(i, 2)))

    place = (lax.div(me, 32), lax.rem(lax.div(me, 8), 4), lax.rem(lax.div(me, 2), 4))

    def ring(i, stage):
        axis = lax.rem(i + stage, 3)
        return jnp.where(axis == 0, 32, jnp.where(axis == 1, 8, 2)), jnp.where(axis == 0, place[0], jnp.where(axis == 1, place[1], place[2]))

    def peer(r, d):
        stride, v = r
        return me + (lax.rem(v + d, 4) - v) * stride

    def send(src, dst, send_sem, recv_sem, to):
        return pltpu.make_async_remote_copy(src_ref=src, dst_ref=dst, send_sem=send_sem, recv_sem=recv_sem,
                                            device_id={"dp": to}, device_id_type=MESH)

    def slots(i):
        j = jnp.where(i == NT - 1, OWN - 1, lax.div(i, 2))
        return j, lax.rem(j, R)

    def c0(i, w):
        j, s = slots(i)
        return [send(b0.at[s, :, pl.ds(0, w)], r0.at[j, :, pl.ds(0, w)], s0.at[s], d0.at[j], mate)]

    def c1a(i, w):
        (j, s), r = slots(i), ring(i, 0)
        return [send(b1a.at[s, pl.ds(FROM[k], HALF[k]), pl.ds(0, w)], r1a.at[j, pl.ds(FROM[k], HALF[k]), pl.ds(0, w)], s1a.at[s, k], d1a.at[j, k], peer(r, d))
                for k, d in ((0, 1), (1, 3))]

    def c1b(i, w):
        (j, s), r = slots(i), ring(i, 0)
        return [send(b1b.at[s, k, :, pl.ds(0, w)], r1b.at[j, k, :, pl.ds(0, w)], s1b.at[s, k], d1b.at[j, k], peer(r, d)) for k, d in ((0, 1), (1, 3))]

    def c2(i, w):
        (j, s), r = slots(i), ring(i, 1)
        return [send(b2.at[s, k, :, pl.ds(0, w)], r2.at[j, k, :, pl.ds(0, w)], s2.at[s, k], d2.at[j, k], peer(r, k + 1)) for k in range(3)]

    def c3(i, w):
        (j, s), r = slots(i), ring(i, 2)
        return [send(r3.at[j, r[1], :, pl.ds(0, w)], r3.at[j, r[1], :, pl.ds(0, w)], s3.at[s, k], d3.at[j, k], peer(r, k + 1)) for k in range(3)]

    def sums(i, start, size, w):
        if w == W:
            return i, rows(start, size, 32), pl.ds(0, W)
        return WHOLE, rows(start, size, 32), pl.ds(pl.multiple_of(128 * (i - WHOLE), 128), w)

    def gather(i, w, start, size, to, ss, rs):
        piece = out.at[sums(i, start, size, w)]
        return send(piece, piece, ss, rs, to)

    def f2(i, w):
        (j, s), x1, x2 = slots(i), ring(i, 0), ring(i, 1)
        return [gather(i, w, 256 * x1[1] + 64 * x2[1], 64, peer(x2, k + 1), t2.at[s, k], e2.at[j, k]) for k in range(3)]

    def f1a(i, w):
        (j, s), x1 = slots(i), ring(i, 0)
        return [gather(i, w, 256 * x1[1], 256, peer(x1, d), t1a.at[s, k], e1a.at[j, k]) for k, d in ((0, 1), (1, 3))]

    def f1b(i, w):
        (j, s), x1 = slots(i), ring(i, 0)
        return [gather(i, w, 256 * lax.rem(x1[1] + 4 - d, 4) + FROM[k], HALF[k], peer(x1, d), t1b.at[s, k], e1b.at[j, k])
                for k, d in ((0, 1), (1, 3))]

    def f0(i, w, which):
        (j, s), x1 = slots(i), ring(i, 0)
        return [gather(i, w, 256 * lax.rem(x1[1] + d, 4), 256, mate, t0.at[s, k], e0.at[i, k])
                for k, d in ((0, 0), (1, 3), (2, 1), (3, 2)) if k in which]

    def start(copies):
        for x in copies:
            x.start()

    def arrived(copies):
        for x in copies:
            x.wait_recv()

    def sent(copies):
        for x in copies:
            x.wait_send()

    def gcopy(i):
        s = lax.rem(i, 2)
        n, j = lax.div(i, PER), lax.rem(i, PER)
        return pltpu.make_async_copy(g_ref.at[0, n, :, pl.ds(pl.multiple_of(j * W, W), W)], gb.at[s], sem_g.at[s])

    def gnarrow(i):
        s = lax.rem(i, 2)
        return pltpu.make_async_copy(g_ref.at[0, i - WHOLE, :, pl.ds(PER * W, 128)], gb.at[s, :, pl.ds(0, 128)], sem_g.at[s])

    def acopy(k):
        s = lax.rem(k, NA)
        n, j = lax.div(k, BLOCKS), lax.rem(k, BLOCKS)
        return pltpu.make_async_copy(a_ref.at[0, n, rows(j * CH, CH, CH)], raw.at[s], sem_a.at[s])

    barrier = pltpu.get_barrier_semaphore()
    pl.semaphore_signal(barrier, inc=1, device_id={"dp": mate}, device_id_type=MESH)
    for axis in range(3):
        for d in (1, 2, 3):
            pl.semaphore_signal(barrier, inc=1, device_id={"dp": peer(ring(axis, 0), d)}, device_id_type=MESH)

    for k in range(NA - 1):
        acopy(k).start()
    gcopy(0).start()

    def transpose(k):
        @pl.when(k + NA - 1 < N * BLOCKS)
        def _():
            acopy(k + NA - 1).start()

        acopy(k).wait()
        n, j = lax.div(k, BLOCKS), lax.rem(k, BLOCKS)
        at[n, :, rows(j * CH, CH, CH)] = raw[lax.rem(k, NA)].T

    def first(k, carry):
        transpose(k)
        return carry

    lax.fori_loop(0, BLOCKS, first, 0)
    pl.semaphore_wait(barrier, 10)

    def tile(i, w, mine):
        _, s = slots(i)
        r = jnp.dot(at[lax.div(i, PER) if w == W else i - WHOLE], gb[lax.rem(i, 2), :, :w], preferred_element_type=F32)
        if mine:
            acc[s, :, :w] = r
        else:
            b0[s, :, :w] = r.astype(BF)
            start(c0(i, w))

    def e_0(i, mine):
        @pl.when(i + 1 < WHOLE)
        def _():
            gcopy(i + 1).start()

        @pl.when((i + 1 >= WHOLE) & (i + 1 < NT))
        def _():
            gnarrow(i + 1).start()

        @pl.when(i < WHOLE)
        def _():
            gcopy(i).wait()

        @pl.when(i >= WHOLE)
        def _():
            gnarrow(i).wait()

        for w, fits in ((W, i < WHOLE), (128, i >= WHOLE)):
            @pl.when(fits & mine)
            def _(w=w):
                tile(i, w, True)

            @pl.when(fits & jnp.logical_not(mine))
            def _(w=w):
                tile(i, w, False)

        @pl.when(i < BLOCKS)
        def _():
            transpose(i + BLOCKS)

    def pair(i, w, at_row, size):
        j, s = slots(i)
        return acc[s, rows(at_row, size, 32), :w] + r0[j, rows(at_row, size, 32), :w].astype(F32)

    def e_1(i, w):
        (j, s), (_, v) = slots(i), ring(i, 0)
        arrived(c0(i, w))
        p = lax.rem(v + 2, 4) * 256
        b1a[s, :, :w] = pair(i, w, p, 256).astype(BF)
        start(c1a(i, w))

    def e_2(i, w):
        (j, s), (_, v) = slots(i), ring(i, 0)
        arrived(c1a(i, w))
        for k, d in ((0, 1), (1, 3)):
            p, o = lax.rem(v + d, 4) * 256, 1 - k
            mine, other = (slice(FROM[x], FROM[x] + HALF[x]) for x in (k, o))
            b1b[s, k, mine, :w] = (pair(i, w, p + FROM[k], HALF[k]) + r1a[j, mine, :w].astype(F32)).astype(BF)
            b1b[s, k, other, :w] = pair(i, w, p + FROM[o], HALF[o]).astype(BF)
        start(c1b(i, w))

    def e_3(i, w):
        (j, s), (_, v), (_, x) = slots(i), ring(i, 0), ring(i, 1)
        sent(c1a(i, w))
        arrived(c1b(i, w))
        q2[s, :, :w] = pair(i, w, v * 256, 256) + r1b[j, 0, :, :w].astype(F32) + r1b[j, 1, :, :w].astype(F32)
        for k in range(3):
            b2[s, k, :, :w] = q2[s, rows(lax.rem(x + k + 1, 4) * 64, 64, 64), :w].astype(BF)
        start(c2(i, w))

    def e_4(i, w):
        (j, s), (_, x), (_, u) = slots(i), ring(i, 1), ring(i, 2)
        sent(c1b(i, w))
        arrived(c2(i, w))
        partial = q2[s, rows(x * 64, 64, 64), :w] + r2[j, 0, :, :w].astype(F32) + r2[j, 1, :, :w].astype(F32) + r2[j, 2, :, :w].astype(F32)
        r3[j, u, :, :w] = partial.astype(BF)
        start(c3(i, w))

    def e_5(i, w):
        (j, s), (_, v), (_, x) = slots(i), ring(i, 0), ring(i, 1)
        sent(c2(i, w))
        arrived(c3(i, w))
        total = r3[j, 0, :, :w].astype(F32) + r3[j, 1, :, :w].astype(F32) + r3[j, 2, :, :w].astype(F32) + r3[j, 3, :, :w].astype(F32)
        out[sums(i, 256 * v + 64 * x, 64, w)] = total.astype(BF)
        start(f2(i, w))

    def e_6(i, w):
        sent(c3(i, w))
        arrived(f2(i, w))
        start(f1a(i, w))
        start(f0(i, w, (0,)))

    def e_7(i, w):
        sent(f2(i, w))
        arrived(f1a(i, w))
        start(f1b(i, w))
        start(f0(i, w, (1, 2)))

    def e_8(i, w):
        sent(f1a(i, w))
        arrived(f1b(i, w))
        start(f0(i, w, (3,)))

    def e_9(i, w):
        sent(f1b(i, w))
        sent(f0(i, w, (0, 1, 2, 3)))

    owned = (e_1, e_2, e_3, e_4, e_5, e_6, e_7, e_8, e_9)

    def iteration(t, carry):
        @pl.when(t < NT)
        def _():
            e_0(t, owner(t) == c)

        for lag, step in zip(LAG[1:], owned):
            i = t - lag
            for w, fits in ((W, (i >= 0) & (i < WHOLE)), (128, (i >= WHOLE) & (i < NT))):
                @pl.when(fits & (owner(i) == c))
                def _(i=i, w=w, step=step):
                    step(i, w)

                if step is e_2 or step is e_9:
                    @pl.when(fits & (owner(i) != c))
                    def _(i=i, w=w, step=step):
                        if step is e_2:
                            sent(c0(i, w))
                        else:
                            arrived(f0(i, w, (0, 1, 2, 3)))

        return carry

    lax.fori_loop(0, NT + LAG[-1], iteration, 0)


def store(x, out, sems):
    copies = [pltpu.make_async_copy(x.at[i], out.at[i // PER, :, pl.ds(i % PER * W, W)], sems.at[i]) for i in range(WHOLE)]
    copies += [pltpu.make_async_copy(x.at[WHOLE, :, pl.ds(128 * n, 128)], out.at[n, :, pl.ds(PER * W, 128)], sems.at[WHOLE + n])
               for n in range(N)]
    for y in copies:
        y.start()
    for y in copies:
        y.wait()


def solution(mesh):
    dma = pltpu.SemaphoreType.DMA

    def step(a, g):
        sums = pl.pallas_call(
            kernel,
            out_shape=pltpu.VMEM((WHOLE + 1, D, W), BF),
            in_specs=[pl.BlockSpec(memory_space=pl.ANY)] * 2,
            out_specs=pl.BlockSpec(memory_space=pltpu.VMEM),
            scratch_shapes=[
                pltpu.VMEM((NA, CH, D), BF), pltpu.VMEM((N, D, T), BF), pltpu.VMEM((2, T, W), BF),
                pltpu.VMEM((R, D, W), F32), pltpu.VMEM((R, 256, W), F32),
                pltpu.VMEM((R, D, W), BF), pltpu.VMEM((R, 256, W), BF), pltpu.VMEM((R, 2, 256, W), BF),
                pltpu.VMEM((R, 3, 64, W), BF),
                pltpu.VMEM((OWN, D, W), BF), pltpu.VMEM((OWN, 256, W), BF), pltpu.VMEM((OWN, 2, 256, W), BF),
                pltpu.VMEM((OWN, 3, 64, W), BF), pltpu.VMEM((OWN, 4, 64, W), BF),
                dma((NA,)), dma((2,)),
                dma((R,)), dma((R, 2)), dma((R, 2)), dma((R, 3)), dma((R, 3)),
                dma((R, 3)), dma((R, 2)), dma((R, 2)), dma((R, 4)),
                dma((OWN,)), dma((OWN, 2)), dma((OWN, 2)), dma((OWN, 3)), dma((OWN, 3)),
                dma((OWN, 3)), dma((OWN, 2)), dma((OWN, 2)), dma((NT, 4)),
            ],
            compiler_params=pltpu.CompilerParams(collective_id=0, has_side_effects=True, vmem_limit_bytes=50 * 1024 * 1024),
        )(a, g)
        return pl.pallas_call(
            store,
            out_shape=jax.ShapeDtypeStruct((N, D, FF), BF),
            in_specs=[pl.BlockSpec(memory_space=pltpu.VMEM)],
            out_specs=pl.BlockSpec(memory_space=pl.ANY),
            scratch_shapes=[dma((NT,))],
            compiler_params=pltpu.CompilerParams(vmem_limit_bytes=1024 * 1024),
        )(sums)

    return jax.shard_map(step, mesh=mesh, in_specs=(P(("rep", "dp")), P(("rep", "dp"))), out_specs=P("rep"), check_vma=False)
```

time: 129 us -> 127 us (0.984)
    pallas_call x1, Pallas kernels: 124 us -> 122 us  [step(): pl.pallas_call(kernel, out_shape=pltpu.VMEM((WHOLE + 1, D, W), BF), in_sp...]
where the time goes in v3:
time: 127 us
  Pallas kernels  127 us (100%)
    pallas_call x1, Pallas kernels, step(): pl.pallas_call(kernel, out_shape=pltpu.VMEM((WHOLE + 1, D, W), BF), in_sp...  122 us
    pallas_call x1, Pallas kernels, step(): pl.pallas_call(store, out_shape=jax.ShapeDtypeStruct((N, D, FF), BF), in_...  4.91 us

profile of v3, /device:TPU:1, one launch (start us, length us, event | category | flops | bytes accessed | tf_op | source)
XLA Modules:
  0.0 126.8 jit_solution(17237822674492154560)
XLA Ops:
  0.0 121.9 %shard_map.28.x = bf16[25,1024,256]{2,1,0:T(8,128)(2,1)S(1)} custom-call(bf16[1,2,4096,1024]{3,2,1,0:T(8,128)(2,1)} %a_ref.1, bf16[1,2,4096,3200]{3,2,1,0:T(8,128)(2,1)} %g_ref.1), custom_call_target="tpu_custom_call" | custom-call | tf_op jit(solution)/shard_map/pallas_call | solution.py:303
  121.9 4.9 %shard_map.29 = bf16[2,1024,3200]{2,1,0:T(8,128)(2,1)} custom-call(bf16[25,1024,256]{2,1,0:T(8,128)(2,1)S(1)} %shard_map.28.x), custom_call_target="tpu_custom_call" | custom-call | tf_op jit(solution)/shard_map/pallas_call | solution.py:323

commit v4 on v3

--- a/solution.py
+++ b/solution.py
@@ -22,36 +22,48 @@
 NA = 4
 
 
+def rem(x, y):
+    return x % y if isinstance(x, int) else lax.rem(x, y)
+
+
+def div(x, y):
+    return x // y if isinstance(x, int) else lax.div(x, y)
+
+
+def pick(which, x, y):
+    return (x if which else y) if isinstance(which, bool) else jnp.where(which, x, y)
+
+
 def rows(start, size, unit):
-    return pl.ds(pl.multiple_of(start, unit), size)
+    return pl.ds(start if isinstance(start, int) else pl.multiple_of(start, unit), size)
 
 
 def kernel(a_ref, g_ref, out, raw, at, gb, acc, q2, b0, b1a, b1b, b2, r0, r1a, r1b, r2, r3,
            sem_a, sem_g, s0, s1a, s1b, s2, s3, t2, t1a, t1b, t0, d0, d1a, d1b, d2, d3, e2, e1a, e1b, e0):
     me = lax.axis_index("dp")
-    c = lax.rem(me, 2)
+    c = rem(me, 2)
     mate = me + 1 - 2 * c
 
     def owner(i):
-        return jnp.where(i >= NT - 3, 1, jnp.where(i == NT - 4, 0, 1 - lax.rem(i, 2)))
-
-    place = (lax.div(me, 32), lax.rem(lax.div(me, 8), 4), lax.rem(lax.div(me, 2), 4))
+        return pick(i >= NT - 3, 1, pick(i == NT - 4, 0, 1 - rem(i, 2)))
+
+    place = (div(me, 32), rem(div(me, 8), 4), rem(div(me, 2), 4))
 
     def ring(i, stage):
-        axis = lax.rem(i + stage, 3)
-        return jnp.where(axis == 0, 32, jnp.where(axis == 1, 8, 2)), jnp.where(axis == 0, place[0], jnp.where(axis == 1, place[1], place[2]))
+        axis = rem(i + stage, 3)
+        return pick(axis == 0, 32, pick(axis == 1, 8, 2)), pick(axis == 0, place[0], pick(axis == 1, place[1], place[2]))
 
     def peer(r, d):
         stride, v = r
-        return me + (lax.rem(v + d, 4) - v) * stride
+        return me + (rem(v + d, 4) - v) * stride
 
     def send(src, dst, send_sem, recv_sem, to):
         return pltpu.make_async_remote_copy(src_ref=src, dst_ref=dst, send_sem=send_sem, recv_sem=recv_sem,
                                             device_id={"dp": to}, device_id_type=MESH)
 
     def slots(i):
-        j = jnp.where(i == NT - 1, OWN - 1, lax.div(i, 2))
-        return j, lax.rem(j, R)
+        j = pick(i == NT - 1, OWN - 1, div(i, 2))
+        return j, rem(j, R)
 
     def c0(i, w):
         j, s = slots(i)
@@ -77,7 +89,7 @@
     def sums(i, start, size, w):
         if w == W:
             return i, rows(start, size, 32), pl.ds(0, W)
-        return WHOLE, rows(start, size, 32), pl.ds(pl.multiple_of(128 * (i - WHOLE), 128), w)
+        return WHOLE, rows(start, size, 32), rows(128 * (i - WHOLE), w, 128)
 
     def gather(i, w, start, size, to, ss, rs):
         piece = out.at[sums(i, start, size, w)]
@@ -93,12 +105,12 @@
 
     def f1b(i, w):
         (j, s), x1 = slots(i), ring(i, 0)
-        return [gather(i, w, 256 * lax.rem(x1[1] + 4 - d, 4) + FROM[k], HALF[k], peer(x1, d), t1b.at[s, k], e1b.at[j, k])
+        return [gather(i, w, 256 * rem(x1[1] + 4 - d, 4) + FROM[k], HALF[k], peer(x1, d), t1b.at[s, k], e1b.at[j, k])
                 for k, d in ((0, 1), (1, 3))]
 
     def f0(i, w, which):
         (j, s), x1 = slots(i), ring(i, 0)
-        return [gather(i, w, 256 * lax.rem(x1[1] + d, 4), 256, mate, t0.at[s, k], e0.at[i, k])
+        return [gather(i, w, 256 * rem(x1[1] + d, 4), 256, mate, t0.at[s, k], e0.at[i, k])
                 for k, d in ((0, 0), (1, 3), (2, 1), (3, 2)) if k in which]
 
     def start(copies):
@@ -114,17 +126,17 @@
             x.wait_send()
 
     def gcopy(i):
-        s = lax.rem(i, 2)
-        n, j = lax.div(i, PER), lax.rem(i, PER)
+        s = rem(i, 2)
+        n, j = div(i, PER), rem(i, PER)
         return pltpu.make_async_copy(g_ref.at[0, n, :, pl.ds(pl.multiple_of(j * W, W), W)], gb.at[s], sem_g.at[s])
 
     def gnarrow(i):
-        s = lax.rem(i, 2)
+        s = rem(i, 2)
         return pltpu.make_async_copy(g_ref.at[0, i - WHOLE, :, pl.ds(PER * W, 128)], gb.at[s, :, pl.ds(0, 128)], sem_g.at[s])
 
     def acopy(k):
-        s = lax.rem(k, NA)
-        n, j = lax.div(k, BLOCKS), lax.rem(k, BLOCKS)
+        s = rem(k, NA)
+        n, j = div(k, BLOCKS), rem(k, BLOCKS)
         return pltpu.make_async_copy(a_ref.at[0, n, rows(j * CH, CH, CH)], raw.at[s], sem_a.at[s])
 
     barrier = pltpu.get_barrier_semaphore()
@@ -143,8 +155,8 @@
             acopy(k + NA - 1).start()
 
         acopy(k).wait()
-        n, j = lax.div(k, BLOCKS), lax.rem(k, BLOCKS)
-        at[n, :, rows(j * CH, CH, CH)] = raw[lax.rem(k, NA)].T
+        n, j = div(k, BLOCKS), rem(k, BLOCKS)
+        at[n, :, rows(j * CH, CH, CH)] = raw[rem(k, NA)].T
 
     def first(k, carry):
         transpose(k)
@@ -155,7 +167,7 @@
 
     def tile(i, w, mine):
         _, s = slots(i)
-        r = jnp.dot(at[lax.div(i, PER) if w == W else i - WHOLE], gb[lax.rem(i, 2), :, :w], preferred_element_type=F32)
+        r = jnp.dot(at[div(i, PER) if w == W else i - WHOLE], gb[rem(i, 2), :, :w], preferred_element_type=F32)
         if mine:
             acc[s, :, :w] = r
         else:
@@ -199,7 +211,7 @@
     def e_1(i, w):
         (j, s), (_, v) = slots(i), ring(i, 0)
         arrived(c0(i, w))
-        p = lax.rem(v + 2, 4) * 256
+        p = rem(v + 2, 4) * 256
         b1a[s, :, :w] = pair(i, w, p, 256).astype(BF)
         start(c1a(i, w))
 
@@ -207,7 +219,7 @@
         (j, s), (_, v) = slots(i), ring(i, 0)
         arrived(c1a(i, w))
         for k, d in ((0, 1), (1, 3)):
-            p, o = lax.rem(v + d, 4) * 256, 1 - k
+            p, o = rem(v + d, 4) * 256, 1 - k
             mine, other = (slice(FROM[x], FROM[x] + HALF[x]) for x in (k, o))
             b1b[s, k, mine, :w] = (pair(i, w, p + FROM[k], HALF[k]) + r1a[j, mine, :w].astype(F32)).astype(BF)
             b1b[s, k, other, :w] = pair(i, w, p + FROM[o], HALF[o]).astype(BF)
@@ -219,7 +231,7 @@
         arrived(c1b(i, w))
         q2[s, :, :w] = pair(i, w, v * 256, 256) + r1b[j, 0, :, :w].astype(F32) + r1b[j, 1, :, :w].astype(F32)
         for k in range(3):
-            b2[s, k, :, :w] = q2[s, rows(lax.rem(x + k + 1, 4) * 64, 64, 64), :w].astype(BF)
+            b2[s, k, :, :w] = q2[s, rows(rem(x + k + 1, 4) * 64, 64, 64), :w].astype(BF)
         start(c2(i, w))
 
     def e_4(i, w):
@@ -262,28 +274,41 @@
     owned = (e_1, e_2, e_3, e_4, e_5, e_6, e_7, e_8, e_9)
 
     def iteration(t, carry):
-        @pl.when(t < NT)
-        def _():
-            e_0(t, owner(t) == c)
-
+        e_0(t, owner(t) == c)
         for lag, step in zip(LAG[1:], owned):
             i = t - lag
-            for w, fits in ((W, (i >= 0) & (i < WHOLE)), (128, (i >= WHOLE) & (i < NT))):
-                @pl.when(fits & (owner(i) == c))
-                def _(i=i, w=w, step=step):
-                    step(i, w)
-
-                if step is e_2 or step is e_9:
-                    @pl.when(fits & (owner(i) != c))
-                    def _(i=i, w=w, step=step):
-                        if step is e_2:
-                            sent(c0(i, w))
-                        else:
-                            arrived(f0(i, w, (0, 1, 2, 3)))
+            inside = (i >= 0) & (i < WHOLE)
+
+            @pl.when(inside & (owner(i) == c))
+            def _(i=i, step=step):
+                step(i, W)
+
+            if step is e_2 or step is e_9:
+                @pl.when(inside & (owner(i) != c))
+                def _(i=i, step=step):
+                    other(i, W, step)
 
         return carry
 
-    lax.fori_loop(0, NT + LAG[-1], iteration, 0)
+    def other(i, w, step):
+        if step is e_2:
+            sent(c0(i, w))
+        elif step is e_9:
+            arrived(f0(i, w, (0, 1, 2, 3)))
+
+    lax.fori_loop(0, NT, iteration, 0)
+
+    for t in range(NT - 1, NT + LAG[-1]):
+        left = [(t - lag, step) for lag, step in zip(LAG[1:], owned) if t - lag < NT and (t >= NT or t - lag >= WHOLE)]
+        for core in (0, 1):
+            @pl.when(c == core)
+            def _(core=core, left=left):
+                for i, step in left:
+                    w = W if i < WHOLE else 128
+                    if owner(i) == core:
+                        step(i, w)
+                    else:
+                        other(i, w, step)
 
 
 def store(x, out, sems):

time: 127 us -> 124 us (0.976)
  Pallas kernels: 127 us -> 124 us
    pallas_call x1, Pallas kernels: 122 us -> 119 us  [step(): pl.pallas_call(kernel, out_shape=pltpu.VMEM((WHOLE + 1, D, W), BF), in_sp...]
where the time goes in v4:
time: 124 us
  Pallas kernels  124 us (100%)
    pallas_call x1, Pallas kernels, step(): pl.pallas_call(kernel, out_shape=pltpu.VMEM((WHOLE + 1, D, W), BF), in_sp...  119 us
    pallas_call x1, Pallas kernels, step(): pl.pallas_call(store, out_shape=jax.ShapeDtypeStruct((N, D, FF), BF), in_...  4.91 us

profile of v4, /device:TPU:1, one launch (start us, length us, event | category | flops | bytes accessed | tf_op | source)
XLA Modules:
  0.0 124.3 jit_solution(598259569417650449)
XLA Ops:
  0.0 119.4 %shard_map.28.x = bf16[25,1024,256]{2,1,0:T(8,128)(2,1)S(1)} custom-call(bf16[1,2,4096,1024]{3,2,1,0:T(8,128)(2,1)} %a_ref.1, bf16[1,2,4096,3200]{3,2,1,0:T(8,128)(2,1)} %g_ref.1), custom_call_target="tpu_custom_call" | custom-call | tf_op jit(solution)/shard_map/pallas_call | solution.py:328
  119.4 4.9 %shard_map.29 = bf16[2,1024,3200]{2,1,0:T(8,128)(2,1)} custom-call(bf16[25,1024,256]{2,1,0:T(8,128)(2,1)S(1)} %shard_map.28.x), custom_call_target="tpu_custom_call" | custom-call | tf_op jit(solution)/shard_map/pallas_call | solution.py:348
